TPU v7x, 32 devices: a whole 2x2x4 slice. The times are simulated.
32 devices in a mesh: ctx: 8 (over z, y), tp: 4 (over x, core).
Axes of the slice: x: 2, y: 2, z: 4, core: 2. Of those that a mesh axis runs over, the one named last changes fastest.
Arguments:
- queries: bfloat16 [2048, 64, 128], P('ctx', 'tp'), may hold values from -48 to 48
- keys: bfloat16 [2048, 8, 128], P('ctx', 'tp'), may hold values from -3 to 3
- values: bfloat16 [2048, 8, 128], P('ctx', 'tp'), may hold values from -6 to 6
- segment_ids: int32 [2048], P('ctx'), may hold values from 0 to 7, never falling along the last dimension, each value on 1 to 1280 neighbouring positions
Outputs:
- attended: bfloat16 [2048, 8192], P(('ctx', 'tp'))
Inputs may be any that keep to these rules, and one draw needn't show every extreme that they name: `segment_ids`: ids never fall along the tokens; each document holds 1 to 1280 tokens, and one holds exactly 1280.
All inputs are finite; a program needn't handle non-finite values.
Results may differ from a plain program's by a relative error of at most 0.003.
Values may be sent and summed in bfloat16 or wider, within the bound.
A program may use at most 64 MiB of HBM per device.

v0:
```python
import math

import jax
import jax.numpy as jnp
from jax import lax
from jax.sharding import PartitionSpec as P


def passed_along(value, axis, by):
    length = lax.axis_size(axis)
    pairs = [(i, i + by) for i in range(length) if 0 <= i + by < length]
    return lax.ppermute(value, axis, pairs)


def attend_rows(state, grouped, seg_q, pos_q, keys, values, seg_k, pos_k, live):
    scale = 1.0 / math.sqrt(grouped.shape[-1])
    high, total, accum = state
    scores = jnp.einsum("tkgd,pkd->kgtp", grouped, keys, preferred_element_type=jnp.float32) * scale
    allowed = (seg_q[:, None] == seg_k[None, :]) & (pos_k[None, :] <= pos_q[:, None]) & live
    scores = jnp.where(allowed, scores, -1e30)
    newtop = jnp.maximum(high, jnp.max(scores, axis=-1))
    factor = jnp.exp(high - newtop)
    weights = jnp.where(allowed, jnp.exp(scores - newtop[..., None]), 0.0)
    total = total * factor + jnp.sum(weights, axis=-1)
    accum = accum * factor[..., None] + jnp.einsum(
        "kgtp,pkd->kgtd", weights.astype(jnp.bfloat16), values, preferred_element_type=jnp.float32
    )
    return (newtop, total, accum)


def fold_piece(state, grouped, seg_q, pos_q, keys, values, seg_k, start, live):
    length = keys.shape[0]
    first = 0 * length
    pos_rows = start + first + lax.iota(jnp.int32, length)
    return attend_rows(state, grouped, seg_q, pos_q, keys, values, seg_k, pos_rows, live)


def local(queries, keys, values, segment_ids):
    rows, heads, head = queries.shape
    groups = keys.shape[1]
    per_group = heads // groups
    ctx_count = lax.axis_size("ctx")
    here = lax.axis_index("ctx")
    grouped = queries.reshape(rows, groups, per_group, head)
    pos_q = here * rows + lax.iota(jnp.int32, rows)
    initial = (
        jnp.full((groups, per_group, rows), -1e30, jnp.float32),
        jnp.zeros((groups, per_group, rows), jnp.float32),
        jnp.zeros((groups, per_group, rows, head), jnp.float32),
    )
    longest = rows * ctx_count * 5 // 8
    reach = min((longest + rows - 1) // rows, ctx_count - 1)
    state = fold_piece(
        initial, grouped, segment_ids, pos_q, keys, values, segment_ids, here * rows, True
    )

    def step(distance, carry):
        state, block = carry
        block = passed_along((block[0], block[1], block[2]), "ctx", 1)
        owner = here - distance
        state = fold_piece(
            state,
            grouped,
            segment_ids,
            pos_q,
            block[0],
            block[1],
            block[2],
            owner * rows,
            owner >= 0,
        )
        return (state, block)

    state, unused = lax.fori_loop(1, reach + 1, step, (state, (keys, values, segment_ids)))
    high, total, accum = state
    result = (accum / total[..., None]).astype(jnp.bfloat16)
    result = jnp.transpose(result, (2, 0, 1, 3)).reshape(rows, heads * head)
    return lax.all_to_all(result, "tp", split_axis=0, concat_axis=1, tiled=True)


def solution(mesh):
    in_specs = (P("ctx", "tp", None), P("ctx", "tp", None), P("ctx", "tp", None), P("ctx"))
    out_specs = P(("ctx", "tp"), None)
    return jax.shard_map(local, mesh=mesh, in_specs=in_specs, out_specs=out_specs, check_vma=False)
```

profile of v0, /device:TPU:0, one launch (start us, length us, event | category | flops | bytes accessed | tf_op | source)
XLA Modules:
  0.0 117.8 jit_solution(8736475935258747422)
XLA Ops:
  0.0 0.7 copy.52
  0.7 0.9 compare_and_fusion
  1.6 1.5 %copy.21 = bf16[256,16,128]{2,0,1:T(8,128)(2,1)S(1)} copy(bf16[256,16,128]{2,1,0:T(8,128)(2,1)} %param.6) | data formatting | bytes 2097152 | tf_op args[0]
  3.1 1.6 %copy.25 = bf16[256,2,128]{2,0,1:T(8,128)(2,1)} copy(bf16[256,2,128]{2,1,0:T(2,128)(2,1)} %param.7) | data formatting | bytes 262144
  4.7 1.7 %fusion.20 = (f32[2,8,256]{2,1,0:T(8,128)S(1)}, f32[2,256,256,8]{2,1,3,0:T(8,128)S(1)}) fusion(pred[256,256]{0,1:T(8,128)(4,1)S(1)} %compare_and_fusion, bf16[256,2,8,128]{3,0,2,1:T(8,128)(2,1)S(1)} %bitcast.62, bf16[256,2,128,1]{2,1,0,3:T(2,128)(2,1)} %bitcast.65), kind=kOutput, calls=%fused_computation.26 | convolution fusion | flops 271577088 | bytes 5455872 | tf_op jit(solution)/shard_map/tkgd,pkd->kgtp/dot_general | solution.py:18
  6.4 1.9 %copy-done = f32[2,256,256,8]{2,1,3,0:T(8,128)} copy-done((f32[2,256,256,8]{2,1,3,0:T(8,128)}, f32[2,256,256,8]{2,1,3,0:T(8,128)S(1)}, u32[]{:S(2)}) %copy-start) | copy-done | bytes 4194328
  8.3 1.0 fusion.22
  9.4 0.7 copy.26
  10.1 3.4 %fusion.30 = f32[2,8,256,128]{3,2,1,0:T(8,128)S(1)} fusion(f32[2,256,256,8]{2,1,3,0:T(8,128)} %copy-done, f32[2,8,256]{2,1,0:T(8,128)S(1)} %broadcast_maximum_fusion, pred[256,256]{0,1:T(8,128)(4,1)S(1)} %compare_and_fusion, f32[2,8,256]{2,1,0:T(8,128)S(1)} %get-tuple-element.278, bf16[256,2,128,1]{2,1,0,3:T(2,128)(2,1)S(1)} %bitcast.66), kind=kOutput, calls=%fused_computation.36 | convolution fusion | flops 274202624 | bytes 6520832 | tf_op jit(solution)/shard_map/kgtp,pkd->kgtd/dot_general | solution.py:25
  13.5 84.3 %while.24 = (s32[]{:T(128)}, f32[2,8,256]{2,1,0:T(8,128)S(1)}, f32[2,8,256]{2,1,0:T(8,128)S(1)}, f32[2,8,256,128]{3,2,1,0:T(8,128)S(1)}, bf16[256,2,128]{2,0,1:T...) while((s32[]{:T(128)}, f32[2,8,256]{2,1,0:T(8,128)S(1)}, ...), condition=%wide.region_5.6_spmd.clone, body=%wide.region_2.5_spmd.clone.sunk | while | flops 551821824 | bytes 20197672 | solution.py:74
  13.5 4.9 %collective-permute-start = (s32[256]{0:T(256)S(1)}, s32[256]{0:T(256)S(1)}, u32[]{:S(2)}, u32[]{:S(2)}) collective-permute-start(s32[256]{0:T(256)S(1)} %get-tuple-element.381), channel_id=1, source_target_pairs={{0,4},{4,8},{8,12},{12,16},{16,20},{20,24},{24,28},{1,5},{5,9},{9,... | collective-permute-start | bytes 3080 | tf_op jit(solution)/shard_map/while/body/eval_jaxpr/ppermute | solution.py:12
  18.4 3.4 %collective-permute-start.1 = (bf16[256,2,128]{2,0,1:T(8,128)(2,1)}, bf16[256,2,128]{2,0,1:T(8,128)(2,1)S(1)}, u32[]{:S(2)}, u32[]{:S(2)}) collective-permute-start(bf16[256,2,128]{2,0,1:T(8,128)(2,1)} %get-tuple-element.379), channel_id=1, source_target_pairs={{0,4},{4,8},{8,12},{12,16},{16,20},{20,24},{24,28},{1,5},{5,9},{9,... | collective-permute-start | bytes 393224 | tf_op jit(solution)/shard_map/while/body/eval_jaxpr/ppermute | solution.py:12
  21.9 3.4 %collective-permute-start.2 = (bf16[256,2,128]{2,0,1:T(8,128)(2,1)}, bf16[256,2,128]{2,0,1:T(8,128)(2,1)S(1)}, u32[]{:S(2)}, u32[]{:S(2)}) collective-permute-start(bf16[256,2,128]{2,0,1:T(8,128)(2,1)} %get-tuple-element.380), channel_id=1, source_target_pairs={{0,4},{4,8},{8,12},{12,16},{16,20},{20,24},{24,28},{1,5},{5,9},{9,... | collective-permute-start | bytes 393224 | tf_op jit(solution)/shard_map/while/body/eval_jaxpr/ppermute | solution.py:12
  25.5 0.8 fusion.51
  26.3 1.0 fusion.52
  27.3 0.7 copy.64
  28.8 1.9 %multiply_add_fusion.5 = f32[2,8,256,128]{3,2,1,0:T(8,128)S(1)} fusion(f32[2,8,256,128]{3,2,1,0:T(8,128)S(1)} %get-tuple-element.378, f32[2,256,256,8]{2,1,3,0:T(8,128)S(1)} %get-tuple-element.358, f32[2,8,256]{2,1,0:T(8,128)S(1)} %max.9, pred[256,256]{0,1:T(8,128)(4,1)S(1)} %and_and_fusion.2, f32[2,8,256]{2,1,0:T(8,128)S(1)} %get-tuple-element.360, ...), kind=kOutput, calls=%fused_computation.7.clone.1 | convolution fusion | flops 274726912 | bytes 8617984 | tf_op jit(solution)/shard_map/while/body/eval_jaxpr/kgtp,pkd->kgtd/dot_general | solution.py:25
  30.6 4.2 %collective-permute-start = (s32[256]{0:T(256)S(1)}, s32[256]{0:T(256)S(1)}, u32[]{:S(2)}, u32[]{:S(2)}) collective-permute-start(s32[256]{0:T(256)S(1)} %get-tuple-element.381), channel_id=1, source_target_pairs={{0,4},{4,8},{8,12},{12,16},{16,20},{20,24},{24,28},{1,5},{5,9},{9,... | collective-permute-start | bytes 3080 | tf_op jit(solution)/shard_map/while/body/eval_jaxpr/ppermute | solution.py:12
  34.9 4.3 %collective-permute-start.1 = (bf16[256,2,128]{2,0,1:T(8,128)(2,1)}, bf16[256,2,128]{2,0,1:T(8,128)(2,1)S(1)}, u32[]{:S(2)}, u32[]{:S(2)}) collective-permute-start(bf16[256,2,128]{2,0,1:T(8,128)(2,1)} %get-tuple-element.379), channel_id=1, source_target_pairs={{0,4},{4,8},{8,12},{12,16},{16,20},{20,24},{24,28},{1,5},{5,9},{9,... | collective-permute-start | bytes 393224 | tf_op jit(solution)/shard_map/while/body/eval_jaxpr/ppermute | solution.py:12
  39.2 2.5 %collective-permute-start.2 = (bf16[256,2,128]{2,0,1:T(8,128)(2,1)}, bf16[256,2,128]{2,0,1:T(8,128)(2,1)S(1)}, u32[]{:S(2)}, u32[]{:S(2)}) collective-permute-start(bf16[256,2,128]{2,0,1:T(8,128)(2,1)} %get-tuple-element.380), channel_id=1, source_target_pairs={{0,4},{4,8},{8,12},{12,16},{16,20},{20,24},{24,28},{1,5},{5,9},{9,... | collective-permute-start | bytes 393224 | tf_op jit(solution)/shard_map/while/body/eval_jaxpr/ppermute | solution.py:12
  42.5 0.8 fusion.51
  43.3 1.0 fusion.52
  44.4 0.7 copy.64
  45.7 1.9 %multiply_add_fusion.5 = f32[2,8,256,128]{3,2,1,0:T(8,128)S(1)} fusion(f32[2,8,256,128]{3,2,1,0:T(8,128)S(1)} %get-tuple-element.378, f32[2,256,256,8]{2,1,3,0:T(8,128)S(1)} %get-tuple-element.358, f32[2,8,256]{2,1,0:T(8,128)S(1)} %max.9, pred[256,256]{0,1:T(8,128)(4,1)S(1)} %and_and_fusion.2, f32[2,8,256]{2,1,0:T(8,128)S(1)} %get-tuple-element.360, ...), kind=kOutput, calls=%fused_computation.7.clone.1 | convolution fusion | flops 274726912 | bytes 8617984 | tf_op jit(solution)/shard_map/while/body/eval_jaxpr/kgtp,pkd->kgtd/dot_general | solution.py:25
  47.6 4.3 %collective-permute-start = (s32[256]{0:T(256)S(1)}, s32[256]{0:T(256)S(1)}, u32[]{:S(2)}, u32[]{:S(2)}) collective-permute-start(s32[256]{0:T(256)S(1)} %get-tuple-element.381), channel_id=1, source_target_pairs={{0,4},{4,8},{8,12},{12,16},{16,20},{20,24},{24,28},{1,5},{5,9},{9,... | collective-permute-start | bytes 3080 | tf_op jit(solution)/shard_map/while/body/eval_jaxpr/ppermute | solution.py:12
  51.9 4.7 %collective-permute-start.1 = (bf16[256,2,128]{2,0,1:T(8,128)(2,1)}, bf16[256,2,128]{2,0,1:T(8,128)(2,1)S(1)}, u32[]{:S(2)}, u32[]{:S(2)}) collective-permute-start(bf16[256,2,128]{2,0,1:T(8,128)(2,1)} %get-tuple-element.379), channel_id=1, source_target_pairs={{0,4},{4,8},{8,12},{12,16},{16,20},{20,24},{24,28},{1,5},{5,9},{9,... | collective-permute-start | bytes 393224 | tf_op jit(solution)/shard_map/while/body/eval_jaxpr/ppermute | solution.py:12
  56.6 2.1 %collective-permute-start.2 = (bf16[256,2,128]{2,0,1:T(8,128)(2,1)}, bf16[256,2,128]{2,0,1:T(8,128)(2,1)S(1)}, u32[]{:S(2)}, u32[]{:S(2)}) collective-permute-start(bf16[256,2,128]{2,0,1:T(8,128)(2,1)} %get-tuple-element.380), channel_id=1, source_target_pairs={{0,4},{4,8},{8,12},{12,16},{16,20},{20,24},{24,28},{1,5},{5,9},{9,... | collective-permute-start | bytes 393224 | tf_op jit(solution)/shard_map/while/body/eval_jaxpr/ppermute | solution.py:12
  59.4 0.8 fusion.51
  60.2 1.0 fusion.52
  62.6 1.9 %multiply_add_fusion.5 = f32[2,8,256,128]{3,2,1,0:T(8,128)S(1)} fusion(f32[2,8,256,128]{3,2,1,0:T(8,128)S(1)} %get-tuple-element.378, f32[2,256,256,8]{2,1,3,0:T(8,128)S(1)} %get-tuple-element.358, f32[2,8,256]{2,1,0:T(8,128)S(1)} %max.9, pred[256,256]{0,1:T(8,128)(4,1)S(1)} %and_and_fusion.2, f32[2,8,256]{2,1,0:T(8,128)S(1)} %get-tuple-element.360, ...), kind=kOutput, calls=%fused_computation.7.clone.1 | convolution fusion | flops 274726912 | bytes 8617984 | tf_op jit(solution)/shard_map/while/body/eval_jaxpr/kgtp,pkd->kgtd/dot_general | solution.py:25
  64.5 4.3 %collective-permute-start = (s32[256]{0:T(256)S(1)}, s32[256]{0:T(256)S(1)}, u32[]{:S(2)}, u32[]{:S(2)}) collective-permute-start(s32[256]{0:T(256)S(1)} %get-tuple-element.381), channel_id=1, source_target_pairs={{0,4},{4,8},{8,12},{12,16},{16,20},{20,24},{24,28},{1,5},{5,9},{9,... | collective-permute-start | bytes 3080 | tf_op jit(solution)/shard_map/while/body/eval_jaxpr/ppermute | solution.py:12
  68.8 5.2 %collective-permute-start.1 = (bf16[256,2,128]{2,0,1:T(8,128)(2,1)}, bf16[256,2,128]{2,0,1:T(8,128)(2,1)S(1)}, u32[]{:S(2)}, u32[]{:S(2)}) collective-permute-start(bf16[256,2,128]{2,0,1:T(8,128)(2,1)} %get-tuple-element.379), channel_id=1, source_target_pairs={{0,4},{4,8},{8,12},{12,16},{16,20},{20,24},{24,28},{1,5},{5,9},{9,... | collective-permute-start | bytes 393224 | tf_op jit(solution)/shard_map/while/body/eval_jaxpr/ppermute | solution.py:12
  74.0 1.9 %collective-permute-start.2 = (bf16[256,2,128]{2,0,1:T(8,128)(2,1)}, bf16[256,2,128]{2,0,1:T(8,128)(2,1)S(1)}, u32[]{:S(2)}, u32[]{:S(2)}) collective-permute-start(bf16[256,2,128]{2,0,1:T(8,128)(2,1)} %get-tuple-element.380), channel_id=1, source_target_pairs={{0,4},{4,8},{8,12},{12,16},{16,20},{20,24},{24,28},{1,5},{5,9},{9,... | collective-permute-start | bytes 393224 | tf_op jit(solution)/shard_map/while/body/eval_jaxpr/ppermute | solution.py:12
  76.1 0.7 collective-permute-done.1
  76.8 0.8 fusion.51
  77.6 1.0 fusion.52
  79.9 1.9 %multiply_add_fusion.5 = f32[2,8,256,128]{3,2,1,0:T(8,128)S(1)} fusion(f32[2,8,256,128]{3,2,1,0:T(8,128)S(1)} %get-tuple-element.378, f32[2,256,256,8]{2,1,3,0:T(8,128)S(1)} %get-tuple-element.358, f32[2,8,256]{2,1,0:T(8,128)S(1)} %max.9, pred[256,256]{0,1:T(8,128)(4,1)S(1)} %and_and_fusion.2, f32[2,8,256]{2,1,0:T(8,128)S(1)} %get-tuple-element.360, ...), kind=kOutput, calls=%fused_computation.7.clone.1 | convolution fusion | flops 274726912 | bytes 8617984 | tf_op jit(solution)/shard_map/while/body/eval_jaxpr/kgtp,pkd->kgtd/dot_general | solution.py:25
  81.8 4.2 %collective-permute-start = (s32[256]{0:T(256)S(1)}, s32[256]{0:T(256)S(1)}, u32[]{:S(2)}, u32[]{:S(2)}) collective-permute-start(s32[256]{0:T(256)S(1)} %get-tuple-element.381), channel_id=1, source_target_pairs={{0,4},{4,8},{8,12},{12,16},{16,20},{20,24},{24,28},{1,5},{5,9},{9,... | collective-permute-start | bytes 3080 | tf_op jit(solution)/shard_map/while/body/eval_jaxpr/ppermute | solution.py:12
  86.1 3.8 %collective-permute-start.1 = (bf16[256,2,128]{2,0,1:T(8,128)(2,1)}, bf16[256,2,128]{2,0,1:T(8,128)(2,1)S(1)}, u32[]{:S(2)}, u32[]{:S(2)}) collective-permute-start(bf16[256,2,128]{2,0,1:T(8,128)(2,1)} %get-tuple-element.379), channel_id=1, source_target_pairs={{0,4},{4,8},{8,12},{12,16},{16,20},{20,24},{24,28},{1,5},{5,9},{9,... | collective-permute-start | bytes 393224 | tf_op jit(solution)/shard_map/while/body/eval_jaxpr/ppermute | solution.py:12
  89.9 1.9 %collective-permute-start.2 = (bf16[256,2,128]{2,0,1:T(8,128)(2,1)}, bf16[256,2,128]{2,0,1:T(8,128)(2,1)S(1)}, u32[]{:S(2)}, u32[]{:S(2)}) collective-permute-start(bf16[256,2,128]{2,0,1:T(8,128)(2,1)} %get-tuple-element.380), channel_id=1, source_target_pairs={{0,4},{4,8},{8,12},{12,16},{16,20},{20,24},{24,28},{1,5},{5,9},{9,... | collective-permute-start | bytes 393224 | tf_op jit(solution)/shard_map/while/body/eval_jaxpr/ppermute | solution.py:12
  92.0 0.7 collective-permute-done.1
  92.7 0.8 fusion.51
  93.5 1.0 fusion.52
  95.9 1.9 %multiply_add_fusion.5 = f32[2,8,256,128]{3,2,1,0:T(8,128)S(1)} fusion(f32[2,8,256,128]{3,2,1,0:T(8,128)S(1)} %get-tuple-element.378, f32[2,256,256,8]{2,1,3,0:T(8,128)S(1)} %get-tuple-element.358, f32[2,8,256]{2,1,0:T(8,128)S(1)} %max.9, pred[256,256]{0,1:T(8,128)(4,1)S(1)} %and_and_fusion.2, f32[2,8,256]{2,1,0:T(8,128)S(1)} %get-tuple-element.360, ...), kind=kOutput, calls=%fused_computation.7.clone.1 | convolution fusion | flops 274726912 | bytes 8617984 | tf_op jit(solution)/shard_map/while/body/eval_jaxpr/kgtp,pkd->kgtd/dot_general | solution.py:25
  97.8 0.7 fusion.33
  98.5 0.7 copy.27
  99.7 17.0 %all_to_all.19 = bf16[4,64,2048]{2,1,0:T(8,128)(2,1)S(1)} all-to-all(bf16[4,64,2048]{2,1,0:T(8,128)(2,1)S(1)} %all_to_all.14), channel_id=1, replica_groups=mesh['ctx'=8,'tp'=4] {'tp'}, dimensions={0} | all-to-all | bytes 2097152 | tf_op jit(solution)/shard_map/all_to_all | solution.py:78
  116.7 1.1 copy.39
  (60 shorter events, 7.8 us)
Async XLA Ops:
  4.7 4.7 %copy-start.1 = (bf16[256,2,128]{2,1,0:T(2,128)(2,1)S(1)}, bf16[256,2,128]{2,1,0:T(2,128)(2,1)}, u32[]{:S(2)}) copy-start(bf16[256,2,128]{2,1,0:T(2,128)(2,1)} %param.8) | copy-start | bytes 393220
  6.4 1.9 %copy-start = (f32[2,256,256,8]{2,1,3,0:T(8,128)}, f32[2,256,256,8]{2,1,3,0:T(8,128)S(1)}, u32[]{:S(2)}) copy-start(f32[2,256,256,8]{2,1,3,0:T(8,128)S(1)} %get-tuple-element.281) | copy-start | bytes 12582916
  10.1 3.4 %copy-start.2 = (s32[256]{0:T(256)S(1)}, s32[256]{0:T(256)}, u32[]{:S(2)}) copy-start(s32[256]{0:T(256)} %param.9) | copy-start | bytes 3076
  13.5 11.8 %collective-permute-start = (s32[256]{0:T(256)S(1)}, s32[256]{0:T(256)S(1)}, u32[]{:S(2)}, u32[]{:S(2)}) collective-permute-start(s32[256]{0:T(256)S(1)} %get-tuple-element.381), channel_id=1, source_target_pairs={{0,4},{4,8},{8,12},{12,16},{16,20},{20,24},{24,28},{1,5},{5,9},{9,... | collective-permute-start | bytes 3080 | tf_op jit(solution)/shard_map/while/body/eval_jaxpr/ppermute | solution.py:12
  18.4 7.1 %collective-permute-start.1 = (bf16[256,2,128]{2,0,1:T(8,128)(2,1)}, bf16[256,2,128]{2,0,1:T(8,128)(2,1)S(1)}, u32[]{:S(2)}, u32[]{:S(2)}) collective-permute-start(bf16[256,2,128]{2,0,1:T(8,128)(2,1)} %get-tuple-element.379), channel_id=1, source_target_pairs={{0,4},{4,8},{8,12},{12,16},{16,20},{20,24},{24,28},{1,5},{5,9},{9,... | collective-permute-start | bytes 393224 | tf_op jit(solution)/shard_map/while/body/eval_jaxpr/ppermute | solution.py:12
  21.9 6.2 %collective-permute-start.2 = (bf16[256,2,128]{2,0,1:T(8,128)(2,1)}, bf16[256,2,128]{2,0,1:T(8,128)(2,1)S(1)}, u32[]{:S(2)}, u32[]{:S(2)}) collective-permute-start(bf16[256,2,128]{2,0,1:T(8,128)(2,1)} %get-tuple-element.380), channel_id=1, source_target_pairs={{0,4},{4,8},{8,12},{12,16},{16,20},{20,24},{24,28},{1,5},{5,9},{9,... | collective-permute-start | bytes 393224 | tf_op jit(solution)/shard_map/while/body/eval_jaxpr/ppermute | solution.py:12
  30.6 11.2 %collective-permute-start = (s32[256]{0:T(256)S(1)}, s32[256]{0:T(256)S(1)}, u32[]{:S(2)}, u32[]{:S(2)}) collective-permute-start(s32[256]{0:T(256)S(1)} %get-tuple-element.381), channel_id=1, source_target_pairs={{0,4},{4,8},{8,12},{12,16},{16,20},{20,24},{24,28},{1,5},{5,9},{9,... | collective-permute-start | bytes 3080 | tf_op jit(solution)/shard_map/while/body/eval_jaxpr/ppermute | solution.py:12
  34.9 7.7 %collective-permute-start.1 = (bf16[256,2,128]{2,0,1:T(8,128)(2,1)}, bf16[256,2,128]{2,0,1:T(8,128)(2,1)S(1)}, u32[]{:S(2)}, u32[]{:S(2)}) collective-permute-start(bf16[256,2,128]{2,0,1:T(8,128)(2,1)} %get-tuple-element.379), channel_id=1, source_target_pairs={{0,4},{4,8},{8,12},{12,16},{16,20},{20,24},{24,28},{1,5},{5,9},{9,... | collective-permute-start | bytes 393224 | tf_op jit(solution)/shard_map/while/body/eval_jaxpr/ppermute | solution.py:12
  39.2 5.8 %collective-permute-start.2 = (bf16[256,2,128]{2,0,1:T(8,128)(2,1)}, bf16[256,2,128]{2,0,1:T(8,128)(2,1)S(1)}, u32[]{:S(2)}, u32[]{:S(2)}) collective-permute-start(bf16[256,2,128]{2,0,1:T(8,128)(2,1)} %get-tuple-element.380), channel_id=1, source_target_pairs={{0,4},{4,8},{8,12},{12,16},{16,20},{20,24},{24,28},{1,5},{5,9},{9,... | collective-permute-start | bytes 393224 | tf_op jit(solution)/shard_map/while/body/eval_jaxpr/ppermute | solution.py:12
  47.6 11.2 %collective-permute-start = (s32[256]{0:T(256)S(1)}, s32[256]{0:T(256)S(1)}, u32[]{:S(2)}, u32[]{:S(2)}) collective-permute-start(s32[256]{0:T(256)S(1)} %get-tuple-element.381), channel_id=1, source_target_pairs={{0,4},{4,8},{8,12},{12,16},{16,20},{20,24},{24,28},{1,5},{5,9},{9,... | collective-permute-start | bytes 3080 | tf_op jit(solution)/shard_map/while/body/eval_jaxpr/ppermute | solution.py:12
  51.9 7.6 %collective-permute-start.1 = (bf16[256,2,128]{2,0,1:T(8,128)(2,1)}, bf16[256,2,128]{2,0,1:T(8,128)(2,1)S(1)}, u32[]{:S(2)}, u32[]{:S(2)}) collective-permute-start(bf16[256,2,128]{2,0,1:T(8,128)(2,1)} %get-tuple-element.379), channel_id=1, source_target_pairs={{0,4},{4,8},{8,12},{12,16},{16,20},{20,24},{24,28},{1,5},{5,9},{9,... | collective-permute-start | bytes 393224 | tf_op jit(solution)/shard_map/while/body/eval_jaxpr/ppermute | solution.py:12
  56.6 5.3 %collective-permute-start.2 = (bf16[256,2,128]{2,0,1:T(8,128)(2,1)}, bf16[256,2,128]{2,0,1:T(8,128)(2,1)S(1)}, u32[]{:S(2)}, u32[]{:S(2)}) collective-permute-start(bf16[256,2,128]{2,0,1:T(8,128)(2,1)} %get-tuple-element.380), channel_id=1, source_target_pairs={{0,4},{4,8},{8,12},{12,16},{16,20},{20,24},{24,28},{1,5},{5,9},{9,... | collective-permute-start | bytes 393224 | tf_op jit(solution)/shard_map/while/body/eval_jaxpr/ppermute | solution.py:12
  64.5 11.4 %collective-permute-start = (s32[256]{0:T(256)S(1)}, s32[256]{0:T(256)S(1)}, u32[]{:S(2)}, u32[]{:S(2)}) collective-permute-start(s32[256]{0:T(256)S(1)} %get-tuple-element.381), channel_id=1, source_target_pairs={{0,4},{4,8},{8,12},{12,16},{16,20},{20,24},{24,28},{1,5},{5,9},{9,... | collective-permute-start | bytes 3080 | tf_op jit(solution)/shard_map/while/body/eval_jaxpr/ppermute | solution.py:12
  68.8 8.0 %collective-permute-start.1 = (bf16[256,2,128]{2,0,1:T(8,128)(2,1)}, bf16[256,2,128]{2,0,1:T(8,128)(2,1)S(1)}, u32[]{:S(2)}, u32[]{:S(2)}) collective-permute-start(bf16[256,2,128]{2,0,1:T(8,128)(2,1)} %get-tuple-element.379), channel_id=1, source_target_pairs={{0,4},{4,8},{8,12},{12,16},{16,20},{20,24},{24,28},{1,5},{5,9},{9,... | collective-permute-start | bytes 393224 | tf_op jit(solution)/shard_map/while/body/eval_jaxpr/ppermute | solution.py:12
  74.0 5.3 %collective-permute-start.2 = (bf16[256,2,128]{2,0,1:T(8,128)(2,1)}, bf16[256,2,128]{2,0,1:T(8,128)(2,1)S(1)}, u32[]{:S(2)}, u32[]{:S(2)}) collective-permute-start(bf16[256,2,128]{2,0,1:T(8,128)(2,1)} %get-tuple-element.380), channel_id=1, source_target_pairs={{0,4},{4,8},{8,12},{12,16},{16,20},{20,24},{24,28},{1,5},{5,9},{9,... | collective-permute-start | bytes 393224 | tf_op jit(solution)/shard_map/while/body/eval_jaxpr/ppermute | solution.py:12
  81.8 10.0 %collective-permute-start = (s32[256]{0:T(256)S(1)}, s32[256]{0:T(256)S(1)}, u32[]{:S(2)}, u32[]{:S(2)}) collective-permute-start(s32[256]{0:T(256)S(1)} %get-tuple-element.381), channel_id=1, source_target_pairs={{0,4},{4,8},{8,12},{12,16},{16,20},{20,24},{24,28},{1,5},{5,9},{9,... | collective-permute-start | bytes 3080 | tf_op jit(solution)/shard_map/while/body/eval_jaxpr/ppermute | solution.py:12
  86.1 6.6 %collective-permute-start.1 = (bf16[256,2,128]{2,0,1:T(8,128)(2,1)}, bf16[256,2,128]{2,0,1:T(8,128)(2,1)S(1)}, u32[]{:S(2)}, u32[]{:S(2)}) collective-permute-start(bf16[256,2,128]{2,0,1:T(8,128)(2,1)} %get-tuple-element.379), channel_id=1, source_target_pairs={{0,4},{4,8},{8,12},{12,16},{16,20},{20,24},{24,28},{1,5},{5,9},{9,... | collective-permute-start | bytes 393224 | tf_op jit(solution)/shard_map/while/body/eval_jaxpr/ppermute | solution.py:12
  89.9 5.3 %collective-permute-start.2 = (bf16[256,2,128]{2,0,1:T(8,128)(2,1)}, bf16[256,2,128]{2,0,1:T(8,128)(2,1)S(1)}, u32[]{:S(2)}, u32[]{:S(2)}) collective-permute-start(bf16[256,2,128]{2,0,1:T(8,128)(2,1)} %get-tuple-element.380), channel_id=1, source_target_pairs={{0,4},{4,8},{8,12},{12,16},{16,20},{20,24},{24,28},{1,5},{5,9},{9,... | collective-permute-start | bytes 393224 | tf_op jit(solution)/shard_map/while/body/eval_jaxpr/ppermute | solution.py:12
where the time goes:
time: 118 us
  starting transfers between devices  55.4 us (47%)
  matrix products  18.3 us (16%)
  blocking collectives  17 us (14%)
  local copies, waits for them, and re-layouts  15.2 us (13%)
  other arithmetic  8.57 us (7%)
  waiting for transfers between devices  2.57 us (2%)
    ppermute x15, starting transfers between devices, passed_along(): return lax.ppermute(value, axis, pairs)  55.4 us
    all_to_all x1, blocking collectives, local(): return lax.all_to_all(result, 'tp', split_axis=0, concat_axis=1, tiled=True)  17 us
    dot_general x6, matrix products, attend_rows(): jnp.einsum('kgtp,pkd->kgtd', weights.astype(jnp.bfloat16), values, prefer...  12.8 us
    while x20, local copies, waits for them, and re-layouts  6.59 us
    unnamed x10, local copies, waits for them, and re-layouts  6.36 us
    reduce_sum x6, other arithmetic, attend_rows(): total = total * factor + jnp.sum(weights, axis=-1)  6.12 us
    dot_general x6, matrix products, attend_rows(): jnp.einsum('tkgd,pkd->kgtp', grouped, keys, preferred_element_type=jnp.fl...  5.53 us
    ppermute x15, waiting for transfers between devices, passed_along(): return lax.ppermute(value, axis, pairs)  2.57 us
  transfers between devices with their start and end apart: 15, of which 5 were waited for; matrix products, arithmetic and copies ran while one was open for 11% of the time, Pallas kernels for 0%

commit v1 on v0

v1 whole, which is shorter than its diff:
```python
import functools
import math

import jax
import jax.numpy as jnp
from jax import lax
from jax.experimental import pallas as pl
from jax.experimental.pallas import tpu as pltpu
from jax.sharding import PartitionSpec as P

MESH = pl.DeviceIdType.MESH
NEG = -1e30


def plane_width(mesh):
    n = mesh.shape["ctx"]
    try:
        width = len({d.coords[1] for d in mesh.devices.flat})
    except Exception:
        width = 2
    return width if n % width == 0 else 1


def kernel(cfg, q_ref, kv_ref, seg_ref, segcol_ref, out_ref,
           buf, segs, bias, acc, top, o_buf,
           kv_send, kv_recv, seg_send, seg_recv, o_send, o_recv, o_local):
    n, ny, reach, tp, groups, per_group, rows, head = cfg
    nz = n // ny
    depth = min(nz - 1, (reach + ny - 1) // ny) + 1
    out_rows = rows // tp
    const = math.log2(math.e) / math.sqrt(head)
    me = lax.axis_index("ctx")
    mt = lax.axis_index("tp")
    z = me // ny
    y = me % ny

    barrier = pltpu.get_barrier_semaphore()
    for d in range(1, reach + 1):
        @pl.when(me + d < n)
        def _():
            pl.semaphore_signal(barrier, inc=1, device_id={"ctx": me + d, "tp": mt}, device_id_type=MESH)

        @pl.when(me - d >= 0)
        def _():
            pl.semaphore_signal(barrier, inc=1, device_id={"ctx": me - d, "tp": mt}, device_id_type=MESH)
    for e in range(1, tp):
        pl.semaphore_signal(barrier, inc=1, device_id={"ctx": me, "tp": (mt + e) % tp}, device_id_type=MESH)
    peers = (tp - 1) + jnp.minimum(n - 1 - me, reach) + jnp.minimum(me, reach)
    pl.semaphore_wait(barrier, peers)

    def piece(s, dy, g, w):
        if s == 0 and dy == 0:
            return kv_ref.at[g, w]
        return buf.at[s * ny + dy, g, w]

    def sem_index(s, dy, g, w):
        return ((s * ny + dy) * groups + g) * 2 + w

    def send_index(s, e, g, w):
        return ((s * ny + e) * groups + g) * 2 + w

    def z_copy(s, g, w):
        return pltpu.make_async_remote_copy(
            src_ref=piece(s, 0, g, w),
            dst_ref=buf.at[(s + 1) * ny, g, w],
            send_sem=kv_send.at[send_index(s, 0, g, w)],
            recv_sem=kv_recv.at[sem_index(s + 1, 0, g, w)],
            device_id={"ctx": me + ny, "tp": mt},
            device_id_type=MESH,
        )

    def y_copy(s, e, g, w):
        return pltpu.make_async_remote_copy(
            src_ref=piece(s, 0, g, w),
            dst_ref=buf.at[s * ny + ny - e, g, w],
            send_sem=kv_send.at[send_index(s, e, g, w)],
            recv_sem=kv_recv.at[sem_index(s, ny - e, g, w)],
            device_id={"ctx": z * ny + (y + e) % ny, "tp": mt},
            device_id_type=MESH,
        )

    def owner(s, dy):
        return (z - s) * ny + (y + dy) % ny

    def has_column(s):
        return (z >= s) & (z * ny - owner(s, 0) <= reach)

    def sends_z(s):
        return (z >= s) & (z + 1 < nz) & ((z + 1) * ny - owner(s, 0) <= reach)

    def sends_y(s, e):
        gap = z * ny + (y + e) % ny - owner(s, 0)
        return (z >= s) & (gap > 0) & (gap <= reach)

    def wanted(s, dy):
        gap = me - owner(s, dy)
        return (z >= s) & (gap > 0) & (gap <= reach)

    def arrived(s, dy, g, w):
        pltpu.make_async_copy(buf.at[s * ny + dy, g, w], buf.at[s * ny + dy, g, w],
                              kv_recv.at[sem_index(s, dy, g, w)]).wait()

    def push(s, g):
        for w in range(2):
            if s > 0:
                @pl.when(has_column(s))
                def _():
                    arrived(s, 0, g, w)
            if s + 1 < depth:
                @pl.when(sends_z(s))
                def _():
                    z_copy(s, g, w).start()
            for e in range(1, ny):
                @pl.when(sends_y(s, e))
                def _():
                    y_copy(s, e, g, w).start()

    def seg_copy(d):
        return pltpu.make_async_remote_copy(
            src_ref=seg_ref,
            dst_ref=segs.at[d],
            send_sem=seg_send.at[d],
            recv_sem=seg_recv.at[d],
            device_id={"ctx": me + d, "tp": mt},
            device_id_type=MESH,
        )

    push(0, 0)
    for d in range(1, reach + 1):
        @pl.when(me + d < n)
        def _():
            seg_copy(d).start()

    def attend(s, dy, g, first):
        k_ref, v_ref = piece(s, dy, g, 0), piece(s, dy, g, 1)
        if first:
            seg_k = seg_ref[...]
        else:
            seg_k = segs[me - owner(s, dy)]
        allowed = segcol_ref[...] == seg_k
        if first:
            r = lax.broadcasted_iota(jnp.int32, (rows, rows), 0)
            c = lax.broadcasted_iota(jnp.int32, (rows, rows), 1)
            allowed = allowed & (c <= r)
        bias[...] = jnp.where(allowed, 0.0, NEG)

        def one(h, carry):
            i = g * per_group + h
            scores = lax.dot_general(q_ref[i], k_ref[...], (((1,), (1,)), ((), ())),
                                     preferred_element_type=jnp.float32)
            scores = scores * const + bias[...]
            high = jnp.max(scores, axis=1, keepdims=True)
            if not first:
                old = top[i][:, :1]
                high = jnp.maximum(old, high)
            weights = jnp.exp2(scores - high).astype(jnp.bfloat16)
            v = jnp.concatenate([v_ref[...], jnp.ones((rows, head), jnp.bfloat16)], axis=1)
            mixed = jnp.dot(weights, v, preferred_element_type=jnp.float32)
            if not first:
                mixed = acc[i] * jnp.exp2(old - high) + mixed
            acc[i] = mixed
            top[i] = jnp.broadcast_to(high, (rows, head))
            return carry

        lax.fori_loop(0, per_group, one, 0, unroll=2)

    def attend_y(s, g):
        for dy in range(1, ny):
            @pl.when(wanted(s, dy))
            def _():
                arrived(s, dy, g, 0)
                arrived(s, dy, g, 1)
                attend(s, dy, g, False)

    per_send = max(per_group // 2, 1)
    width = per_send * head
    pieces = per_group // per_send

    def o_copy(c, e):
        col = pl.multiple_of((mt * groups * pieces + c) * width, width)
        to = (mt + e) % tp
        return pltpu.make_async_remote_copy(
            src_ref=o_buf.at[pl.ds(pl.multiple_of(to * out_rows, out_rows), out_rows), pl.ds(c * width, width)],
            dst_ref=out_ref.at[:, pl.ds(col, width)],
            send_sem=o_send.at[c * tp + e],
            recv_sem=o_recv.at[c * tp + e],
            device_id={"ctx": me, "tp": to},
            device_id_type=MESH,
        )

    def o_own(c):
        col = pl.multiple_of((mt * groups * pieces + c) * width, width)
        return pltpu.make_async_copy(
            o_buf.at[pl.ds(pl.multiple_of(mt * out_rows, out_rows), out_rows), pl.ds(c * width, width)],
            out_ref.at[:, pl.ds(col, width)],
            o_local.at[c],
        )

    def finish(g):
        for p in range(pieces):
            c = g * pieces + p
            for h in range(per_send):
                i = g * per_group + p * per_send + h
                o_buf[:, i * head:(i + 1) * head] = (acc[i, :, :head] / acc[i, :, head:]).astype(jnp.bfloat16)
            for e in range(1, tp):
                o_copy(c, e).start()
            o_own(c).start()

    for g in range(groups):
        attend(0, 0, g, True)
        if g == 0:
            for d in range(1, reach + 1):
                @pl.when(me - d >= 0)
                def _():
                    pltpu.make_async_copy(segs.at[d], segs.at[d], seg_recv.at[d]).wait()
        for s in range(1, depth):
            push(s, g)
            if s == depth - 1 and g + 1 < groups:
                push(0, g + 1)

            @pl.when(wanted(s, 0))
            def _():
                attend(s, 0, g, False)
            attend_y(s - 1, g)
        if depth == 1 and g + 1 < groups:
            push(0, g + 1)
        attend_y(depth - 1, g)
        finish(g)

    for s in range(depth):
        for g in range(groups):
            for w in range(2):
                if s + 1 < depth:
                    @pl.when(sends_z(s))
                    def _():
                        z_copy(s, g, w).wait_send()
                for e in range(1, ny):
                    @pl.when(sends_y(s, e))
                    def _():
                        y_copy(s, e, g, w).wait_send()
    for d in range(1, reach + 1):
        @pl.when(me + d < n)
        def _():
            seg_copy(d).wait_send()
    for c in range(groups * pieces):
        o_own(c).wait()
        for e in range(1, tp):
            o_copy(c, e).wait()


def local(ny, queries, keys, values, segment_ids):
    rows, heads, head = queries.shape
    groups = keys.shape[1]
    per_group = heads // groups
    n = lax.axis_size("ctx")
    tp = lax.axis_size("tp")
    nz = n // ny
    longest = rows * n * 5 // 8
    reach = min((longest + rows - 1) // rows, n - 1)
    depth = min(nz - 1, (reach + ny - 1) // ny) + 1
    q = jnp.transpose(queries, (1, 0, 2))
    kv = jnp.transpose(jnp.stack([keys, values]), (2, 0, 1, 3))
    pieces = groups * (per_group // max(per_group // 2, 1))
    slots = depth * ny
    vmem = pl.BlockSpec(memory_space=pltpu.VMEM)
    dma = pltpu.SemaphoreType.DMA
    cfg = (n, ny, reach, tp, groups, per_group, rows, head)
    return pl.pallas_call(
        functools.partial(kernel, cfg),
        out_shape=jax.ShapeDtypeStruct((rows // tp, tp * heads * head), jnp.bfloat16),
        in_specs=[vmem] * 4,
        out_specs=vmem,
        scratch_shapes=[
            pltpu.VMEM((slots, groups, 2, rows, head), jnp.bfloat16),
            pltpu.VMEM((reach + 1, 1, rows), jnp.int32),
            pltpu.VMEM((rows, rows), jnp.float32),
            pltpu.VMEM((heads, rows, 2 * head), jnp.float32),
            pltpu.VMEM((heads, rows, head), jnp.float32),
            pltpu.VMEM((rows, heads * head), jnp.bfloat16),
            dma((slots * groups * 2,)),
            dma((slots * groups * 2,)),
            dma((reach + 1,)),
            dma((reach + 1,)),
            dma((pieces * tp,)),
            dma((pieces * tp,)),
            dma((pieces,)),
        ],
        compiler_params=pltpu.CompilerParams(
            collective_id=0, has_side_effects=True, vmem_limit_bytes=56 * 1024 * 1024
        ),
    )(q, kv, segment_ids.reshape(1, rows), segment_ids.reshape(rows, 1))


def solution(mesh):
    in_specs = (P("ctx", "tp", None), P("ctx", "tp", None), P("ctx", "tp", None), P("ctx"))
    out_specs = P(("ctx", "tp"), None)
    body = functools.partial(local, plane_width(mesh))
    return jax.shard_map(body, mesh=mesh, in_specs=in_specs, out_specs=out_specs, check_vma=False)
```

time: 118 us -> 65.1 us (0.55)
  the two profiles are of different devices: /device:TPU:0 before, /device:TPU:25 now
where the time goes in v1:
time: 65.1 us; the launch traced here: 64.9 us
  Pallas kernels  58.1 us (89%)
  local copies, waits for them, and re-layouts  6.03 us (9%)
  other arithmetic  0.73 us (1%)
    pallas_call x1, Pallas kernels, local(): pl.pallas_call(functools.partial(kernel, cfg), out_shape=jax.ShapeDtypeSt...  58.1 us
    unnamed x6, local copies, waits for them, and re-layouts  3.51 us
    reshape x1, local copies, waits for them, and re-layouts, local(): segment_ids.reshape(rows, 1)  1.58 us

profile of v1, /device:TPU:25, one launch (start us, length us, event | category | flops | bytes accessed | tf_op | source)
XLA Modules:
  0.0 64.9 jit_solution(14744195171425018176)
XLA Ops:
  0.0 0.0 copy-start.1
  0.0 0.0 copy-start
  0.0 1.6 %copy.11.segcol_ref = s32[256,1]{1,0:T(8,128)} copy(s32[256,1]{0,1:T(1,128)} %bitcast.12) | data formatting | bytes 2048 | tf_op jit(solution)/shard_map/reshape | solution.py:291
  1.6 0.0 copy-done.1
  1.6 0.9 %copy_bitcast_fusion.1 = (bf16[1,256,2,128]{3,1,0,2:T(8,128)(2,1)S(1)}, bf16[1,256,2,128]{3,1,0,2:T(8,128)(2,1)S(1)}) fusion(bf16[256,2,128]{2,1,0:T(2,128)(2,1)S(1)} %copy-done.1, bf16[256,2,128]{2,1,0:T(2,128)(2,1)} %param.5), kind=kLoop, calls=%fused_computation.2 | loop fusion | bytes 524288 | tf_op jit(solution)/shard_map/stack | solution.py:262
  2.5 0.7 %maximum_bitcast_fusion.kv_ref = bf16[2,2,256,128]{3,2,1,0:T(8,128)(2,1)} fusion(bf16[1,256,2,128]{3,1,0,2:T(8,128)(2,1)S(1)} %get-tuple-element.5, bf16[1,256,2,128]{3,1,0,2:T(8,128)(2,1)S(1)} %get-tuple-element.6), kind=kLoop, calls=%fused_computation.1 | loop fusion | flops 131072 | bytes 524288 | tf_op jit(solution)/shard_map/transpose | solution.py:262
  3.3 0.0 copy-done
  3.3 1.2 %copy.15 = bf16[256,16,128]{2,0,1:T(8,128)(2,1)} copy(bf16[256,16,128]{2,1,0:T(8,128)(2,1)S(1)} %copy-done) | data formatting | bytes 2097152 | tf_op args[0]
  4.5 58.1 %shard_map.46 = bf16[64,8192]{1,0:T(8,128)(2,1)} custom-call(bf16[16,256,128]{2,1,0:T(8,128)(2,1)} %bitcast.11, bf16[2,2,256,128]{3,2,1,0:T(8,128)(2,1)} %maximum_bitcast_fusion.kv_ref, s32[1,256]{1,0:T(1,128)} %bitcast.13, s32[256,1]{1,0:T(8,128)} %copy.11.segcol_ref), custom_call_target="tpu_custom_call" | custom-call | tf_op jit(solution)/shard_map/pallas_call | solution.py:268
  62.6 2.3 %copy.17 = bf16[64,8192]{1,0:T(8,128)(2,1)} copy(bf16[64,8192]{1,0:T(8,128)(2,1)} %shard_map.46) | data formatting | bytes 2097152
Async XLA Ops:
  0.0 1.6 %copy-start.1 = (bf16[256,2,128]{2,1,0:T(2,128)(2,1)S(1)}, bf16[256,2,128]{2,1,0:T(2,128)(2,1)}, u32[]{:S(2)}) copy-start(bf16[256,2,128]{2,1,0:T(2,128)(2,1)} %param.6) | copy-start | bytes 393220
  0.0 3.3 %copy-start = (bf16[256,16,128]{2,1,0:T(8,128)(2,1)S(1)}, bf16[256,16,128]{2,1,0:T(8,128)(2,1)}, u32[]{:S(2)}) copy-start(bf16[256,16,128]{2,1,0:T(8,128)(2,1)} %param.4) | copy-start | bytes 3145732

commit v2 on v1

--- a/solution.py
+++ b/solution.py
@@ -21,8 +21,8 @@
     return width if n % width == 0 else 1
 
 
-def kernel(cfg, q_ref, kv_ref, seg_ref, segcol_ref, out_ref,
-           buf, segs, bias, acc, top, o_buf,
+def kernel(cfg, q_ref, k_in, v_in, seg_ref, out_ref,
+           buf, segs, segcol, bias, acc, top, o_buf,
            kv_send, kv_recv, seg_send, seg_recv, o_send, o_recv, o_local):
     n, ny, reach, tp, groups, per_group, rows, head = cfg
     nz = n // ny
@@ -50,7 +50,7 @@
 
     def piece(s, dy, g, w):
         if s == 0 and dy == 0:
-            return kv_ref.at[g, w]
+            return (k_in, v_in)[w].at[g]
         return buf.at[s * ny + dy, g, w]
 
     def sem_index(s, dy, g, w):
@@ -131,13 +131,16 @@
         def _():
             seg_copy(d).start()
 
+    segcol[...] = jnp.transpose(jnp.broadcast_to(seg_ref[...], (head, rows)))
+
     def attend(s, dy, g, first):
         k_ref, v_ref = piece(s, dy, g, 0), piece(s, dy, g, 1)
         if first:
             seg_k = seg_ref[...]
         else:
             seg_k = segs[me - owner(s, dy)]
-        allowed = segcol_ref[...] == seg_k
+        column = segcol[...]
+        allowed = jnp.concatenate([column] * (rows // head), axis=1) == seg_k
         if first:
             r = lax.broadcasted_iota(jnp.int32, (rows, rows), 0)
             c = lax.broadcasted_iota(jnp.int32, (rows, rows), 1)
@@ -149,20 +152,21 @@
             scores = lax.dot_general(q_ref[i], k_ref[...], (((1,), (1,)), ((), ())),
                                      preferred_element_type=jnp.float32)
             scores = scores * const + bias[...]
-            high = jnp.max(scores, axis=1, keepdims=True)
+            high = jnp.broadcast_to(jnp.max(scores, axis=1, keepdims=True), (rows, head))
             if not first:
-                old = top[i][:, :1]
+                old = top[i]
                 high = jnp.maximum(old, high)
-            weights = jnp.exp2(scores - high).astype(jnp.bfloat16)
+            weights = jnp.exp2(scores - jnp.concatenate([high] * (rows // head), axis=1)).astype(jnp.bfloat16)
             v = jnp.concatenate([v_ref[...], jnp.ones((rows, head), jnp.bfloat16)], axis=1)
             mixed = jnp.dot(weights, v, preferred_element_type=jnp.float32)
             if not first:
-                mixed = acc[i] * jnp.exp2(old - high) + mixed
+                factor = jnp.exp2(old - high)
+                mixed = acc[i] * jnp.concatenate([factor, factor], axis=1) + mixed
             acc[i] = mixed
-            top[i] = jnp.broadcast_to(high, (rows, head))
+            top[i] = high
             return carry
 
-        lax.fori_loop(0, per_group, one, 0, unroll=2)
+        lax.fori_loop(0, per_group, one, 0, unroll=per_group)
 
     def attend_y(s, g):
         for dy in range(1, ny):
@@ -259,7 +263,8 @@
     reach = min((longest + rows - 1) // rows, n - 1)
     depth = min(nz - 1, (reach + ny - 1) // ny) + 1
     q = jnp.transpose(queries, (1, 0, 2))
-    kv = jnp.transpose(jnp.stack([keys, values]), (2, 0, 1, 3))
+    k = jnp.transpose(keys, (1, 0, 2))
+    v = jnp.transpose(values, (1, 0, 2))
     pieces = groups * (per_group // max(per_group // 2, 1))
     slots = depth * ny
     vmem = pl.BlockSpec(memory_space=pltpu.VMEM)
@@ -273,6 +278,7 @@
         scratch_shapes=[
             pltpu.VMEM((slots, groups, 2, rows, head), jnp.bfloat16),
             pltpu.VMEM((reach + 1, 1, rows), jnp.int32),
+            pltpu.VMEM((rows, head), jnp.int32),
             pltpu.VMEM((rows, rows), jnp.float32),
             pltpu.VMEM((heads, rows, 2 * head), jnp.float32),
             pltpu.VMEM((heads, rows, head), jnp.float32),
@@ -288,7 +294,7 @@
         compiler_params=pltpu.CompilerParams(
             collective_id=0, has_side_effects=True, vmem_limit_bytes=56 * 1024 * 1024
         ),
-    )(q, kv, segment_ids.reshape(1, rows), segment_ids.reshape(rows, 1))
+    )(q, k, v, segment_ids.reshape(1, rows))
 
 
 def solution(mesh):

time: 65.1 us -> 47.7 us (0.73)
  Pallas kernels: 58.1 us -> 41.1 us
  other arithmetic: 0.73 us -> 0 us
    pallas_call x1, Pallas kernels: 58.1 us -> 41.1 us  [local(): pl.pallas_call(functools.partial(kernel, cfg), out_shape=jax.ShapeDtypeSt...]
    transpose x0 -> x1, local copies, waits for them, and re-layouts: none -> 1.71 us  [local(): v = jnp.transpose(values, (1, 0, 2))]
    reshape x1 -> x0, local copies, waits for them, and re-layouts: 1.58 us -> none  [local(): segment_ids.reshape(rows, 1)]
    unnamed x6 -> x2, local copies, waits for them, and re-layouts: 3.51 us -> 4.73 us
    another operation x1 -> x0, local copies, waits for them, and re-layouts: 0.94 us -> none  [local(): kv = jnp.transpose(jnp.stack([keys, values]), (2, 0, 1, 3))]
    transpose x1 -> x0, other arithmetic: 0.73 us -> none  [local(): kv = jnp.transpose(jnp.stack([keys, values]), (2, 0, 1, 3))]
where the time goes in v2:
time: 47.7 us; the launch traced here: 47.5 us
  Pallas kernels  41.1 us (86%)
  local copies, waits for them, and re-layouts  6.44 us (14%)
    pallas_call x1, Pallas kernels, local(): pl.pallas_call(functools.partial(kernel, cfg), out_shape=jax.ShapeDtypeSt...  41.1 us
    unnamed x2, local copies, waits for them, and re-layouts  4.73 us
    transpose x1, local copies, waits for them, and re-layouts, local(): v = jnp.transpose(values, (1, 0, 2))  1.71 us

profile of v2, /device:TPU:25, one launch (start us, length us, event | category | flops | bytes accessed | tf_op | source)
XLA Modules:
  0.0 47.5 jit_solution(2140912509996013225)
XLA Ops:
  0.0 1.7 %copy_bitcast_fusion.1 = (bf16[2,256,128]{2,1,0:T(8,128)(2,1)}, bf16[2,256,128]{2,1,0:T(8,128)(2,1)}) fusion(bf16[256,2,128]{2,1,0:T(2,128)(2,1)} %param.6, bf16[256,2,128]{2,1,0:T(2,128)(2,1)} %param.5), kind=kLoop, calls=%fused_computation.1 | loop fusion | bytes 524288 | tf_op jit(solution)/shard_map/transpose | solution.py:267
  1.7 2.5 %copy.11 = bf16[256,16,128]{2,0,1:T(8,128)(2,1)} copy(bf16[256,16,128]{2,1,0:T(8,128)(2,1)} %param.4) | data formatting | bytes 2097152 | tf_op args[0]
  4.2 41.1 %shard_map.46 = bf16[64,8192]{1,0:T(8,128)(2,1)} custom-call(bf16[16,256,128]{2,1,0:T(8,128)(2,1)} %bitcast.8, bf16[2,256,128]{2,1,0:T(8,128)(2,1)} %get-tuple-element.6.k_in, bf16[2,256,128]{2,1,0:T(8,128)(2,1)} %get-tuple-element.5.v_in, s32[1,256]{1,0:T(1,128)} %bitcast.9), custom_call_target="tpu_custom_call" | custom-call | tf_op jit(solution)/shard_map/pallas_call | solution.py:273
  45.2 2.3 %copy.13 = bf16[64,8192]{1,0:T(8,128)(2,1)} copy(bf16[64,8192]{1,0:T(8,128)(2,1)} %shard_map.46) | data formatting | bytes 2097152

commit v3 on v2

--- a/solution.py
+++ b/solution.py
@@ -21,8 +21,8 @@
     return width if n % width == 0 else 1
 
 
-def kernel(cfg, q_ref, k_in, v_in, seg_ref, out_ref,
-           buf, segs, segcol, bias, acc, top, o_buf,
+def kernel(cfg, q_in, k_in, v_in, seg_ref, out_ref,
+           q_ref, buf, segs, segcol, bias, acc, top, o_buf,
            kv_send, kv_recv, seg_send, seg_recv, o_send, o_recv, o_local):
     n, ny, reach, tp, groups, per_group, rows, head = cfg
     nz = n // ny
@@ -79,18 +79,35 @@
             device_id_type=MESH,
         )
 
+    last = depth - 1
+    straight = last >= 2 and last * ny > reach
+
+    def far_copy(dy, g, w):
+        return pltpu.make_async_remote_copy(
+            src_ref=piece(last - 1, dy, g, w),
+            dst_ref=buf.at[last * ny + dy, g, w],
+            send_sem=kv_send.at[send_index(last, dy, g, w)],
+            recv_sem=kv_recv.at[sem_index(last, dy, g, w)],
+            device_id={"ctx": me + ny, "tp": mt},
+            device_id_type=MESH,
+        )
+
+    def sends_far(dy):
+        gap = me + ny - owner(last - 1, dy)
+        return (z >= last - 1) & (z + 1 < nz) & (gap <= reach)
+
     def owner(s, dy):
         return (z - s) * ny + (y + dy) % ny
 
     def has_column(s):
-        return (z >= s) & (z * ny - owner(s, 0) <= reach)
+        return (z >= s) & (s * ny <= reach)
 
     def sends_z(s):
-        return (z >= s) & (z + 1 < nz) & ((z + 1) * ny - owner(s, 0) <= reach)
+        return (z >= s) & (z + 1 < nz) & ((s + 1) * ny <= reach)
 
     def sends_y(s, e):
         gap = z * ny + (y + e) % ny - owner(s, 0)
-        return (z >= s) & (gap > 0) & (gap <= reach)
+        return (z >= s) & (s * ny <= reach) & (gap > 0) & (gap <= reach)
 
     def wanted(s, dy):
         gap = me - owner(s, dy)
@@ -131,6 +148,8 @@
         def _():
             seg_copy(d).start()
 
+    for i in range(groups * per_group):
+        q_ref[i] = q_in[:, i, :]
     segcol[...] = jnp.transpose(jnp.broadcast_to(seg_ref[...], (head, rows)))
 
     def attend(s, dy, g, first):
@@ -174,6 +193,11 @@
             def _():
                 arrived(s, dy, g, 0)
                 arrived(s, dy, g, 1)
+                if straight and s == last - 1:
+                    @pl.when(sends_far(dy))
+                    def _():
+                        far_copy(dy, g, 0).start()
+                        far_copy(dy, g, 1).start()
                 attend(s, dy, g, False)
 
     per_send = max(per_group // 2, 1)
@@ -242,6 +266,13 @@
                     @pl.when(sends_y(s, e))
                     def _():
                         y_copy(s, e, g, w).wait_send()
+    if straight:
+        for g in range(groups):
+            for w in range(2):
+                for dy in range(1, ny):
+                    @pl.when(wanted(last - 1, dy) & sends_far(dy))
+                    def _():
+                        far_copy(dy, g, w).wait_send()
     for d in range(1, reach + 1):
         @pl.when(me + d < n)
         def _():
@@ -262,7 +293,6 @@
     longest = rows * n * 5 // 8
     reach = min((longest + rows - 1) // rows, n - 1)
     depth = min(nz - 1, (reach + ny - 1) // ny) + 1
-    q = jnp.transpose(queries, (1, 0, 2))
     k = jnp.transpose(keys, (1, 0, 2))
     v = jnp.transpose(values, (1, 0, 2))
     pieces = groups * (per_group // max(per_group // 2, 1))
@@ -276,6 +306,7 @@
         in_specs=[vmem] * 4,
         out_specs=vmem,
         scratch_shapes=[
+            pltpu.VMEM((heads, rows, head), jnp.bfloat16),
             pltpu.VMEM((slots, groups, 2, rows, head), jnp.bfloat16),
             pltpu.VMEM((reach + 1, 1, rows), jnp.int32),
             pltpu.VMEM((rows, head), jnp.int32),
@@ -294,7 +325,7 @@
         compiler_params=pltpu.CompilerParams(
             collective_id=0, has_side_effects=True, vmem_limit_bytes=56 * 1024 * 1024
         ),
-    )(q, k, v, segment_ids.reshape(1, rows))
+    )(queries, k, v, segment_ids.reshape(1, rows))
 
 
 def solution(mesh):

time: 47.7 us -> 41.9 us (0.88)
  Pallas kernels: 41.1 us -> 37.8 us
  local copies, waits for them, and re-layouts: 6.44 us -> 3.96 us
    pallas_call x1, Pallas kernels: 41.1 us -> 37.8 us  [local(): pl.pallas_call(functools.partial(kernel, cfg), out_shape=jax.ShapeDtypeSt...]
    unnamed x2 -> x1, local copies, waits for them, and re-layouts: 4.73 us -> 2.26 us
where the time goes in v3:
time: 41.9 us; the launch traced here: 41.7 us
  Pallas kernels  37.8 us (90%)
  local copies, waits for them, and re-layouts  3.96 us (9%)
    pallas_call x1, Pallas kernels, local(): pl.pallas_call(functools.partial(kernel, cfg), out_shape=jax.ShapeDtypeSt...  37.8 us
    unnamed x1, local copies, waits for them, and re-layouts  2.26 us
    transpose x1, local copies, waits for them, and re-layouts, local(): v = jnp.transpose(values, (1, 0, 2))  1.7 us

profile of v3, /device:TPU:25, one launch (start us, length us, event | category | flops | bytes accessed | tf_op | source)
XLA Modules:
  0.0 41.7 jit_solution(10725232607453252559)
XLA Ops:
  0.0 1.7 %copy_bitcast_fusion = (bf16[2,256,128]{2,1,0:T(8,128)(2,1)}, bf16[2,256,128]{2,1,0:T(8,128)(2,1)}) fusion(bf16[256,2,128]{2,1,0:T(2,128)(2,1)} %param.6, bf16[256,2,128]{2,1,0:T(2,128)(2,1)} %param.5), kind=kLoop, calls=%fused_computation | loop fusion | bytes 524288 | tf_op jit(solution)/shard_map/transpose | solution.py:297
  1.7 37.8 %shard_map.46 = bf16[64,8192]{1,0:T(8,128)(2,1)} custom-call(bf16[256,16,128]{2,1,0:T(8,128)(2,1)} %q_in.1, bf16[2,256,128]{2,1,0:T(8,128)(2,1)} %get-tuple-element.6.k_in, bf16[2,256,128]{2,1,0:T(8,128)(2,1)} %get-tuple-element.5.v_in, s32[1,256]{1,0:T(1,128)} %bitcast.5), custom_call_target="tpu_custom_call" | custom-call | tf_op jit(solution)/shard_map/pallas_call | solution.py:303
  39.5 2.3 %copy.10 = bf16[64,8192]{1,0:T(8,128)(2,1)} copy(bf16[64,8192]{1,0:T(8,128)(2,1)} %shard_map.46) | data formatting | bytes 2097152
